TPU v7x, 128 devices: a whole 4x4x4 slice. The times are simulated.
128 devices in a mesh: ops: 32 (over z, y, core), site: 4 (over x).
Axes of the slice: x: 4, y: 4, z: 4, core: 2. Of those that a mesh axis runs over, the one named last changes fastest.
Arguments:
- wavefunction: bfloat16 [2048, 2048], replicated, may hold values from -6 to 6
- left_blocks: bfloat16 [256, 16, 192, 192], P('ops', 'site'), may hold values from -0.4375 to 0.4375
- right_blocks: bfloat16 [256, 16, 192, 192], P('ops', 'site'), may hold values from -0.078125 to 0.078125
- left_sector: int32 [2048], replicated, may hold values from 0 to 15, as said below
- right_sector: int32 [2048], replicated, may hold values from 0 to 15, as said below
- term_count: int32 [32], P('ops'), may hold values from 1 to 8, as said below
- left_energy: float32 [2048], replicated, may hold values from -1 to 1
- right_energy: float32 [2048], replicated, may hold values from -1 to 1
- subspace: bfloat16 [2, 16, 192, 2048], P(None, 'site'), may hold values from -0.0078125 to 0.0078125
Outputs:
- sigma: bfloat16 [16, 192, 2048], P('site')
- projections: float32 [2], replicated
Inputs may be any that keep to these rules, and one draw needn't show every extreme that they name: `left_sector`: sector ids never fall along the bond; each of the 16 sectors has 1 to 192 states and one has exactly 192. `right_sector`: sector ids never fall along the bond; each of the 16 sectors has 1 to 192 states and one has exactly 192. `term_count`: some group has all 8 slots live.
All inputs are finite; a program needn't handle non-finite values.
Results may differ from a plain program's by a relative error of at most 0.0045.
Values may be sent and summed in bfloat16 or wider, within the bound.
No kernel may reach another device: no remote copies, remote signals or barrier semaphores. Data moves between devices by JAX's collectives and lax.ppermute only.
A program may use at most 192 MiB of HBM per device.

v0:
```python
import jax
import jax.numpy as jnp
from jax import lax
from jax.sharding import PartitionSpec as P


def from_everyone(value, axis):
    size = lax.axis_size(axis)
    return lax.all_to_all(
        jnp.broadcast_to(value[None], (size, *value.shape)), axis, 0, 0, tiled=True
    )


def over_copies(value, axis):
    return from_everyone(value, axis).sum(axis=0)


def sector_tables(sector_ids, sectors):
    labels = jnp.arange(sectors, dtype=jnp.int32)
    sector_starts = jnp.sum((sector_ids[None, :] < labels[:, None]).astype(jnp.int32), axis=1)
    sector_sizes = jnp.sum((sector_ids[None, :] == labels[:, None]).astype(jnp.int32), axis=1)
    return (sector_starts, sector_sizes)


def block_mask(size_now, widest):
    inside = jnp.arange(widest, dtype=jnp.int32) < size_now
    return inside[:, None] & inside[None, :]


def correlations(vectors, values):
    return jnp.sum(vectors.astype(jnp.float32) * values[None], axis=(1, 2, 3))


def local(
    wavefunction,
    left_blocks,
    right_blocks,
    left_sector,
    right_sector,
    term_count,
    left_energy,
    right_energy,
    subspace,
):
    slot_count = left_blocks.shape[0]
    sec_dev = left_blocks.shape[1]
    widest = left_blocks.shape[2]
    bond_dim = wavefunction.shape[0]
    row_count = sec_dev * widest
    sectors = sec_dev * lax.axis_size("site")
    left_start, left_size = sector_tables(left_sector, sectors)
    right_start, right_size = sector_tables(right_sector, sectors)
    active = term_count[0]
    first_sector = lax.axis_index("site") * sec_dev
    psi_padded = jnp.concatenate(
        [wavefunction, jnp.zeros((widest, bond_dim), wavefunction.dtype)], axis=0
    )
    energy_padded = jnp.concatenate([left_energy, jnp.zeros((widest,), jnp.float32)])
    psi_slabs = []
    energies = []
    left_masks = []
    inside_rows = []
    for within in range(sec_dev):
        sector = first_sector + within
        row_start = left_start[sector]
        size_now = left_size[sector]
        psi_slabs.append(lax.dynamic_slice_in_dim(psi_padded, row_start, widest, 0))
        energies.append(lax.dynamic_slice_in_dim(energy_padded, row_start, widest, 0))
        inside = jnp.arange(widest, dtype=jnp.int32) < size_now
        inside_rows.append(inside)
        left_masks.append(inside[:, None] & inside[None, :])

    def left_term(term_idx, stacked):
        blocks = lax.dynamic_index_in_dim(left_blocks, term_idx, 0, False)
        pieces = []
        for within in range(sec_dev):
            masked = jnp.where(left_masks[within], blocks[within], jnp.zeros((), blocks.dtype))
            pieces.append(jnp.dot(masked, psi_slabs[within], preferred_element_type=jnp.float32))
        left_image = jnp.concatenate(pieces, axis=0).astype(jnp.bfloat16)
        left_image = jnp.concatenate(
            [left_image, jnp.zeros((row_count, widest), jnp.bfloat16)], axis=1
        )
        return lax.dynamic_update_index_in_dim(stacked, left_image, term_idx, 0)

    images = lax.fori_loop(
        0, active, left_term, jnp.zeros((slot_count, row_count, bond_dim + widest), jnp.bfloat16)
    )
    part_blocks = lax.all_gather(right_blocks, "site", axis=1, tiled=True)

    def one_sector(within, summed):
        col_start = right_start[within]
        keep_mask = block_mask(right_size[within], widest)
        blocks = lax.dynamic_index_in_dim(part_blocks, within, 1, False)

        def add_term(term_idx, running):
            window = lax.dynamic_slice_in_dim(
                lax.dynamic_index_in_dim(images, term_idx, 0, False), col_start, widest, 1
            )
            one_block = jnp.where(
                keep_mask,
                lax.dynamic_index_in_dim(blocks, term_idx, 0, False),
                jnp.zeros((), blocks.dtype),
            )
            return running + lax.dot_general(
                window, one_block, (((1,), (1,)), ((), ())), preferred_element_type=jnp.float32
            )

        added = lax.fori_loop(0, active, add_term, jnp.zeros((row_count, widest), jnp.float32))
        previous = lax.dynamic_slice_in_dim(summed, col_start, widest, 1)
        return lax.dynamic_update_slice_in_dim(summed, previous + added, col_start, 1)

    folded = lax.fori_loop(
        0, part_blocks.shape[1], one_sector, jnp.zeros((row_count, bond_dim + widest), jnp.float32)
    )
    partial_value = folded[:, :bond_dim].reshape(sec_dev, widest, bond_dim)
    psi_mine = jnp.where(
        jnp.stack(inside_rows)[:, :, None],
        jnp.stack(psi_slabs).astype(jnp.float32),
        jnp.float32(0.0),
    )
    energy_mine = jnp.stack(energies)
    diagonal = (energy_mine[:, :, None] + right_energy[None, None, :]) * psi_mine
    sigma_full = lax.psum(partial_value, "ops") + diagonal
    sigma_out = sigma_full.astype(jnp.bfloat16)
    projections = over_copies(correlations(subspace, sigma_full), "site")
    return (sigma_out, projections)


def solution(mesh):
    in_specs = (
        P(),
        P("ops", "site", None, None),
        P("ops", "site", None, None),
        P(),
        P(),
        P("ops"),
        P(),
        P(),
        P(None, "site", None, None),
    )
    out_specs = (P("site", None, None), P())
    return jax.shard_map(local, mesh=mesh, in_specs=in_specs, out_specs=out_specs, check_vma=False)
```

profile of v0, /device:TPU:24, one launch (start us, length us, event | category | flops | bytes accessed | tf_op | source)
XLA Modules:
  0.0 715.6 jit_solution(18417771134688194427)
XLA Ops:
  7.2 3.9 copy.17
  22.2 5.3 pad_dynamic-slice_fusion
  27.5 9.9 %broadcast_in_dim.39 = bf16[8,768,2240]{2,1,0:T(8,128)(2,1)} broadcast(bf16[]{:T(256)} %constant.184.clone.1), dimensions={} | broadcast | bytes 27525122 | tf_op jit(solution)/shard_map/broadcast_in_dim | solution.py:86
  37.4 40.1 %while.63 = (s32[]{:T(128)}, bf16[8,768,2240]{2,1,0:T(8,128)(2,1)}, s32[]{:T(128)}, bf16[8,4,192,192]{3,2,1,0:T(8,128)(2,1)}, bf16[192,2048]{1,0:T(8,128)(2,1)},...) while((s32[]{:T(128)}, bf16[8,768,2240]{2,1,0:T(8,128)(2,1)}, ...), condition=%wide.region_5.6_spmd.clone, body=%wide.region_4.5_spmd.clone.sunk | while | flops 628211712 | bytes 13373707 | solution.py:85
  53.7 3.3 fusion.67
  63.5 3.4 fusion.67
  73.4 3.4 fusion.67
  77.5 54.4 %all-gather.2.cloned.1.call-done = bf16[8,16,192,192]{3,2,0,1:T(8,128)(2,1)} async-done(((bf16[8,4,192,192]{3,2,0,1:T(8,128)(2,1)}), bf16[8,16,192,192]{3,2,0,1:T(8,128)(2,1)}) %all-gather.2.cloned.1.call-update) | async-done | bytes 9437200 | tf_op jit(solution)/shard_map/all_gather | solution.py:88
  131.9 3.3 broadcast_in_dim.38
  135.2 292.4 %while.62 = (s32[]{:T(128)}, f32[768,2240]{0,1:T(8,128)}, s32[16]{0:T(128)S(1)}, bf16[8,16,192,192]{3,2,0,1:T(8,128)(2,1)}, s32[16]{0:T(128)S(1)}, /*index=5*/s3...) while((s32[]{:T(128)}, f32[768,2240]{0,1:T(8,128)}, ...), condition=%wide.region_9.10_spmd, body=%wide.region_6.9_spmd.sunk | while | flops 56991944 | bytes 6391994 | solution.py:112
  140.3 9.1 %while.64 = (s32[]{:T(128)}, f32[768,192]{0,1:T(8,128)S(1)}, s32[]{:T(128)}, bf16[8,768,2240]{2,1,0:T(8,128)(2,1)}, s32[]{:T(128)}, /*index=5*/bf16[8,192,192]{2...) while((s32[]{:T(128)}, f32[768,192]{0,1:T(8,128)S(1)}, ...), condition=%wide.region_8.8_spmd.clone, body=%wide.region_7.7_spmd.clone.sunk | while | flops 56844292 | bytes 1672871 | solution.py:108
  158.5 9.1 %while.64 = (s32[]{:T(128)}, f32[768,192]{0,1:T(8,128)S(1)}, s32[]{:T(128)}, bf16[8,768,2240]{2,1,0:T(8,128)(2,1)}, s32[]{:T(128)}, /*index=5*/bf16[8,192,192]{2...) while((s32[]{:T(128)}, f32[768,192]{0,1:T(8,128)S(1)}, ...), condition=%wide.region_8.8_spmd.clone, body=%wide.region_7.7_spmd.clone.sunk | while | flops 56844292 | bytes 1672871 | solution.py:108
  176.8 9.1 %while.64 = (s32[]{:T(128)}, f32[768,192]{0,1:T(8,128)S(1)}, s32[]{:T(128)}, bf16[8,768,2240]{2,1,0:T(8,128)(2,1)}, s32[]{:T(128)}, /*index=5*/bf16[8,192,192]{2...) while((s32[]{:T(128)}, f32[768,192]{0,1:T(8,128)S(1)}, ...), condition=%wide.region_8.8_spmd.clone, body=%wide.region_7.7_spmd.clone.sunk | while | flops 56844292 | bytes 1672871 | solution.py:108
  195.1 9.1 %while.64 = (s32[]{:T(128)}, f32[768,192]{0,1:T(8,128)S(1)}, s32[]{:T(128)}, bf16[8,768,2240]{2,1,0:T(8,128)(2,1)}, s32[]{:T(128)}, /*index=5*/bf16[8,192,192]{2...) while((s32[]{:T(128)}, f32[768,192]{0,1:T(8,128)S(1)}, ...), condition=%wide.region_8.8_spmd.clone, body=%wide.region_7.7_spmd.clone.sunk | while | flops 56844292 | bytes 1672871 | solution.py:108
  213.4 9.1 %while.64 = (s32[]{:T(128)}, f32[768,192]{0,1:T(8,128)S(1)}, s32[]{:T(128)}, bf16[8,768,2240]{2,1,0:T(8,128)(2,1)}, s32[]{:T(128)}, /*index=5*/bf16[8,192,192]{2...) while((s32[]{:T(128)}, f32[768,192]{0,1:T(8,128)S(1)}, ...), condition=%wide.region_8.8_spmd.clone, body=%wide.region_7.7_spmd.clone.sunk | while | flops 56844292 | bytes 1672871 | solution.py:108
  231.6 9.1 %while.64 = (s32[]{:T(128)}, f32[768,192]{0,1:T(8,128)S(1)}, s32[]{:T(128)}, bf16[8,768,2240]{2,1,0:T(8,128)(2,1)}, s32[]{:T(128)}, /*index=5*/bf16[8,192,192]{2...) while((s32[]{:T(128)}, f32[768,192]{0,1:T(8,128)S(1)}, ...), condition=%wide.region_8.8_spmd.clone, body=%wide.region_7.7_spmd.clone.sunk | while | flops 56844292 | bytes 1672871 | solution.py:108
  249.9 9.1 %while.64 = (s32[]{:T(128)}, f32[768,192]{0,1:T(8,128)S(1)}, s32[]{:T(128)}, bf16[8,768,2240]{2,1,0:T(8,128)(2,1)}, s32[]{:T(128)}, /*index=5*/bf16[8,192,192]{2...) while((s32[]{:T(128)}, f32[768,192]{0,1:T(8,128)S(1)}, ...), condition=%wide.region_8.8_spmd.clone, body=%wide.region_7.7_spmd.clone.sunk | while | flops 56844292 | bytes 1672871 | solution.py:108
  268.2 9.1 %while.64 = (s32[]{:T(128)}, f32[768,192]{0,1:T(8,128)S(1)}, s32[]{:T(128)}, bf16[8,768,2240]{2,1,0:T(8,128)(2,1)}, s32[]{:T(128)}, /*index=5*/bf16[8,192,192]{2...) while((s32[]{:T(128)}, f32[768,192]{0,1:T(8,128)S(1)}, ...), condition=%wide.region_8.8_spmd.clone, body=%wide.region_7.7_spmd.clone.sunk | while | flops 56844292 | bytes 1672871 | solution.py:108
  286.5 9.1 %while.64 = (s32[]{:T(128)}, f32[768,192]{0,1:T(8,128)S(1)}, s32[]{:T(128)}, bf16[8,768,2240]{2,1,0:T(8,128)(2,1)}, s32[]{:T(128)}, /*index=5*/bf16[8,192,192]{2...) while((s32[]{:T(128)}, f32[768,192]{0,1:T(8,128)S(1)}, ...), condition=%wide.region_8.8_spmd.clone, body=%wide.region_7.7_spmd.clone.sunk | while | flops 56844292 | bytes 1672871 | solution.py:108
  304.7 9.1 %while.64 = (s32[]{:T(128)}, f32[768,192]{0,1:T(8,128)S(1)}, s32[]{:T(128)}, bf16[8,768,2240]{2,1,0:T(8,128)(2,1)}, s32[]{:T(128)}, /*index=5*/bf16[8,192,192]{2...) while((s32[]{:T(128)}, f32[768,192]{0,1:T(8,128)S(1)}, ...), condition=%wide.region_8.8_spmd.clone, body=%wide.region_7.7_spmd.clone.sunk | while | flops 56844292 | bytes 1672871 | solution.py:108
  323.0 9.1 %while.64 = (s32[]{:T(128)}, f32[768,192]{0,1:T(8,128)S(1)}, s32[]{:T(128)}, bf16[8,768,2240]{2,1,0:T(8,128)(2,1)}, s32[]{:T(128)}, /*index=5*/bf16[8,192,192]{2...) while((s32[]{:T(128)}, f32[768,192]{0,1:T(8,128)S(1)}, ...), condition=%wide.region_8.8_spmd.clone, body=%wide.region_7.7_spmd.clone.sunk | while | flops 56844292 | bytes 1672871 | solution.py:108
  341.3 9.1 %while.64 = (s32[]{:T(128)}, f32[768,192]{0,1:T(8,128)S(1)}, s32[]{:T(128)}, bf16[8,768,2240]{2,1,0:T(8,128)(2,1)}, s32[]{:T(128)}, /*index=5*/bf16[8,192,192]{2...) while((s32[]{:T(128)}, f32[768,192]{0,1:T(8,128)S(1)}, ...), condition=%wide.region_8.8_spmd.clone, body=%wide.region_7.7_spmd.clone.sunk | while | flops 56844292 | bytes 1672871 | solution.py:108
  359.6 9.1 %while.64 = (s32[]{:T(128)}, f32[768,192]{0,1:T(8,128)S(1)}, s32[]{:T(128)}, bf16[8,768,2240]{2,1,0:T(8,128)(2,1)}, s32[]{:T(128)}, /*index=5*/bf16[8,192,192]{2...) while((s32[]{:T(128)}, f32[768,192]{0,1:T(8,128)S(1)}, ...), condition=%wide.region_8.8_spmd.clone, body=%wide.region_7.7_spmd.clone.sunk | while | flops 56844292 | bytes 1672871 | solution.py:108
  377.8 9.1 %while.64 = (s32[]{:T(128)}, f32[768,192]{0,1:T(8,128)S(1)}, s32[]{:T(128)}, bf16[8,768,2240]{2,1,0:T(8,128)(2,1)}, s32[]{:T(128)}, /*index=5*/bf16[8,192,192]{2...) while((s32[]{:T(128)}, f32[768,192]{0,1:T(8,128)S(1)}, ...), condition=%wide.region_8.8_spmd.clone, body=%wide.region_7.7_spmd.clone.sunk | while | flops 56844292 | bytes 1672871 | solution.py:108
  396.1 9.1 %while.64 = (s32[]{:T(128)}, f32[768,192]{0,1:T(8,128)S(1)}, s32[]{:T(128)}, bf16[8,768,2240]{2,1,0:T(8,128)(2,1)}, s32[]{:T(128)}, /*index=5*/bf16[8,192,192]{2...) while((s32[]{:T(128)}, f32[768,192]{0,1:T(8,128)S(1)}, ...), condition=%wide.region_8.8_spmd.clone, body=%wide.region_7.7_spmd.clone.sunk | while | flops 56844292 | bytes 1672871 | solution.py:108
  414.4 9.1 %while.64 = (s32[]{:T(128)}, f32[768,192]{0,1:T(8,128)S(1)}, s32[]{:T(128)}, bf16[8,768,2240]{2,1,0:T(8,128)(2,1)}, s32[]{:T(128)}, /*index=5*/bf16[8,192,192]{2...) while((s32[]{:T(128)}, f32[768,192]{0,1:T(8,128)S(1)}, ...), condition=%wide.region_8.8_spmd.clone, body=%wide.region_7.7_spmd.clone.sunk | while | flops 56844292 | bytes 1672871 | solution.py:108
  427.6 5.8 slice.19
  433.5 6.6 copy.18
  442.9 246.8 %all-reduce.5.cloned.1.call-done = f32[4,192,2048]{2,1,0:T(8,128)} async-done(((f32[4,192,2048]{2,1,0:T(8,128)}), f32[4,192,2048]{2,1,0:T(8,128)}) %all-reduce.5.cloned.1.call-update) | async-done | bytes 6291472 | tf_op jit(solution)/shard_map/psum | solution.py:123
  689.7 4.7 fusion.49
  694.4 4.6 multiply_reduce_fusion
  698.9 9.3 %all_to_all.6 = f32[4,1,2]{2,1,0:T(1,128)S(1)} all-to-all(f32[4,1,2]{2,1,0:T(1,128)S(1)} %broadcast_in_dim.42), channel_id=1, replica_groups=mesh['ops'=32,'site'=4] {'site'}, dimensions={0} | all-to-all | bytes 64 | tf_op jit(solution)/shard_map/all_to_all | solution.py:9
  (225 shorter events, 240.5 us)
Async XLA Ops:
  7.2 4.0 copy-start.4
  7.2 14.8 %copy-start.5 = (s32[2048]{0:T(1024)S(1)}, s32[2048]{0:T(1024)}, u32[]{:S(2)}) copy-start(s32[2048]{0:T(1024)} %param.19) | copy-start | bytes 24580
  7.2 124.7 %all-gather.2.cloned.1.call-start = ((), (), s32[]{:S(2)}) async-start(), calls=%async_computation.1 | async-start | bytes 15728640 | tf_op jit(solution)/shard_map/all_gather | solution.py:88
  11.1 678.5 %all-reduce.5.cloned.1.call-start = ((), (), s32[]{:S(2)}) async-start(), calls=%async_computation.2 | async-start | bytes 12582912 | tf_op jit(solution)/shard_map/psum | solution.py:123
  440.1 2.7 copy-start.3
  440.1 249.5 %copy-start = (bf16[192,2048]{1,0:T(8,128)(2,1)S(1)}, bf16[192,2048]{1,0:T(8,128)(2,1)}, u32[]{:S(2)}) copy-start(bf16[192,2048]{1,0:T(8,128)(2,1)} %get-tuple-element.834) | copy-start | bytes 2359300
  440.1 249.5 %copy-start.1 = (bf16[192,2048]{1,0:T(8,128)(2,1)S(1)}, bf16[192,2048]{1,0:T(8,128)(2,1)}, u32[]{:S(2)}) copy-start(bf16[192,2048]{1,0:T(8,128)(2,1)} %get-tuple-element.835) | copy-start | bytes 2359300
  440.1 249.5 %copy-start.2 = (f32[2048]{0:T(1024)S(1)}, f32[2048]{0:T(1024)}, u32[]{:S(2)}) copy-start(f32[2048]{0:T(1024)} %param.22) | copy-start | bytes 24580
Sparse Core Ops, SparseCore 0:
  11.3 120.6 all-gather.1
  440.3 249.3 all-reduce.4
where the time goes:
time: 727 us; the launch traced here: 716 us
  waiting for transfers between devices  301 us (41%)
  local copies, waits for them, and re-layouts  121 us (17%)
  matrix products  116 us (16%)
  loops' own time  88.7 us (12%)
  other arithmetic  57.3 us (8%)
  between operations  21.6 us (3%)
  blocking collectives  9.32 us (1%)
    psum x1, waiting for transfers between devices, local(): sigma_full = lax.psum(partial_value, 'ops') + diagonal  247 us
    dot_general x64, matrix products, add_term(): lax.dot_general(window, one_block, (((1,), (1,)), ((), ())), preferred_el...  92.6 us
    all_gather x1, waiting for transfers between devices, local(): part_blocks = lax.all_gather(right_blocks, 'site', axis=1, tiled=True)  54.4 us
    another operation x16, loops' own time, one_sector(): lax.fori_loop(0, active, add_term, jnp.zeros((row_count, widest), jnp.flo...  53.6 us
    dynamic_update_slice x16, local copies, waits for them, and re-layouts, one_sector(): lax.dynamic_update_slice_in_dim(summed, previous + added, col_start, 1)  47.3 us
    another operation x1, loops' own time, local(): lax.fori_loop(0, part_blocks.shape[1], one_sector, jnp.zeros((row_count,...  31.6 us
    dot_general x16, matrix products, left_term(): jnp.dot(masked, psi_slabs[within], preferred_element_type=jnp.float32)  23.3 us
    squeeze x16, local copies, waits for them, and re-layouts, one_sector(): blocks = lax.dynamic_index_in_dim(part_blocks, within, 1, False)  19.1 us
  transfers between devices with their start and end apart: 2, of which 2 were waited for; matrix products, arithmetic and copies ran while one was open for 8% of the time, Pallas kernels for 0%

commit v1 on v0

--- a/solution.py
+++ b/solution.py
@@ -2,6 +2,13 @@
 import jax.numpy as jnp
 from jax import lax
 from jax.sharding import PartitionSpec as P
+
+
+def gather_over(x, axis, dim):
+    size = lax.axis_size(axis)
+    blocks = jnp.stack([x for _ in range(size)])
+    blocks = lax.all_to_all(blocks, axis, split_axis=0, concat_axis=0)
+    return jnp.concatenate(blocks, axis=dim)
 
 
 def from_everyone(value, axis):
@@ -85,7 +92,7 @@
     images = lax.fori_loop(
         0, active, left_term, jnp.zeros((slot_count, row_count, bond_dim + widest), jnp.bfloat16)
     )
-    part_blocks = lax.all_gather(right_blocks, "site", axis=1, tiled=True)
+    part_blocks = gather_over(right_blocks, "site", 1)
 
     def one_sector(within, summed):
         col_start = right_start[within]

time: 727 us -> 755 us (1.039)
  waiting for transfers between devices: 301 us -> 319 us
    all_to_all x0 -> x1, waiting for transfers between devices: none -> 73.8 us  [gather_over(): blocks = lax.all_to_all(blocks, axis, split_axis=0, concat_axis=0)]
    all_gather x1 -> x0, waiting for transfers between devices: 54.4 us -> none  [local(): part_blocks = lax.all_gather(right_blocks, 'site', axis=1, tiled=True)]
where the time goes in v1:
time: 755 us; the launch traced here: 743 us
  waiting for transfers between devices  319 us (42%)
  local copies, waits for them, and re-layouts  126 us (17%)
  matrix products  116 us (15%)
  loops' own time  88 us (12%)
  other arithmetic  56.5 us (7%)
  between operations  21.6 us (3%)
  blocking collectives  9.32 us (1%)
    psum x1, waiting for transfers between devices, local(): sigma_full = lax.psum(partial_value, 'ops') + diagonal  245 us
    dot_general x64, matrix products, add_term(): lax.dot_general(window, one_block, (((1,), (1,)), ((), ())), preferred_el...  92.6 us
    all_to_all x1, waiting for transfers between devices, gather_over(): blocks = lax.all_to_all(blocks, axis, split_axis=0, concat_axis=0)  73.8 us
    another operation x16, loops' own time, one_sector(): lax.fori_loop(0, active, add_term, jnp.zeros((row_count, widest), jnp.flo...  53.6 us
    dynamic_update_slice x16, local copies, waits for them, and re-layouts, one_sector(): lax.dynamic_update_slice_in_dim(summed, previous + added, col_start, 1)  47.3 us
    another operation x1, loops' own time, local(): lax.fori_loop(0, part_blocks.shape[1], one_sector, jnp.zeros((row_count,...  30.9 us
    dot_general x16, matrix products, left_term(): jnp.dot(masked, psi_slabs[within], preferred_element_type=jnp.float32)  23.2 us
    squeeze x16, local copies, waits for them, and re-layouts, one_sector(): blocks = lax.dynamic_index_in_dim(part_blocks, within, 1, False)  19.1 us
  transfers between devices with their start and end apart: 2, of which 2 were waited for; matrix products, arithmetic and copies ran while one was open for 8% of the time, Pallas kernels for 0%

profile of v1, /device:TPU:24, one launch (start us, length us, event | category | flops | bytes accessed | tf_op | source)
XLA Modules:
  0.0 743.4 jit_solution(13401848723885093831)
XLA Ops:
  9.3 6.2 stack.44
  15.4 6.5 all-to-all-start
  33.0 4.9 pad_dynamic-slice_fusion
  38.0 9.4 %broadcast_in_dim.39 = bf16[8,768,2240]{2,1,0:T(8,128)(2,1)} broadcast(bf16[]{:T(256)} %constant.184.clone.1), dimensions={} | broadcast | bytes 27525122 | tf_op jit(solution)/shard_map/broadcast_in_dim | solution.py:93
  47.4 39.8 %while.63 = (s32[]{:T(128)}, bf16[8,768,2240]{2,1,0:T(8,128)(2,1)}, s32[]{:T(128)}, bf16[8,4,192,192]{3,2,1,0:T(8,128)(2,1)}, bf16[192,2048]{1,0:T(8,128)(2,1)},...) while((s32[]{:T(128)}, bf16[8,768,2240]{2,1,0:T(8,128)(2,1)}, ...), condition=%wide.region_5.6_spmd.clone, body=%wide.region_4.5_spmd.clone.sunk | while | flops 628211712 | bytes 13373707 | solution.py:92
  63.7 3.3 fusion.67
  73.5 3.3 fusion.67
  87.2 73.8 %all-to-all-done = bf16[4,8,4,192,192]{4,3,1,2,0:T(8,128)(2,1)} async-done(((bf16[4,8,4,192,192]{4,3,1,2,0:T(8,128)(2,1)}), bf16[4,8,4,192,192]{4,3,1,2,0:T(8,128)(2,1)}, u32[]{:S(2)}, u32[]{:S(2)}) %all-to-all-start) | async-done | bytes 9437216 | tf_op jit(solution)/shard_map/all_to_all | solution.py:10
  161.0 3.3 broadcast_in_dim.38
  164.3 292.5 %while.62 = (s32[]{:T(128)}, f32[768,2240]{0,1:T(8,128)}, s32[16]{0:T(128)S(1)}, bf16[8,16,192,192]{3,2,0,1:T(8,128)(2,1)}, s32[16]{0:T(128)S(1)}, /*index=5*/s3...) while((s32[]{:T(128)}, f32[768,2240]{0,1:T(8,128)}, ...), condition=%wide.region_9.10_spmd, body=%wide.region_6.9_spmd.sunk | while | flops 56991944 | bytes 6391994 | solution.py:119
  169.4 9.1 %while.64 = (s32[]{:T(128)}, f32[768,192]{0,1:T(8,128)S(1)}, s32[]{:T(128)}, bf16[8,768,2240]{2,1,0:T(8,128)(2,1)}, s32[]{:T(128)}, /*index=5*/bf16[8,192,192]{2...) while((s32[]{:T(128)}, f32[768,192]{0,1:T(8,128)S(1)}, ...), condition=%wide.region_8.8_spmd.clone, body=%wide.region_7.7_spmd.clone.sunk | while | flops 56844292 | bytes 1672871 | solution.py:115
  187.6 9.1 %while.64 = (s32[]{:T(128)}, f32[768,192]{0,1:T(8,128)S(1)}, s32[]{:T(128)}, bf16[8,768,2240]{2,1,0:T(8,128)(2,1)}, s32[]{:T(128)}, /*index=5*/bf16[8,192,192]{2...) while((s32[]{:T(128)}, f32[768,192]{0,1:T(8,128)S(1)}, ...), condition=%wide.region_8.8_spmd.clone, body=%wide.region_7.7_spmd.clone.sunk | while | flops 56844292 | bytes 1672871 | solution.py:115
  205.9 9.1 %while.64 = (s32[]{:T(128)}, f32[768,192]{0,1:T(8,128)S(1)}, s32[]{:T(128)}, bf16[8,768,2240]{2,1,0:T(8,128)(2,1)}, s32[]{:T(128)}, /*index=5*/bf16[8,192,192]{2...) while((s32[]{:T(128)}, f32[768,192]{0,1:T(8,128)S(1)}, ...), condition=%wide.region_8.8_spmd.clone, body=%wide.region_7.7_spmd.clone.sunk | while | flops 56844292 | bytes 1672871 | solution.py:115
  224.2 9.1 %while.64 = (s32[]{:T(128)}, f32[768,192]{0,1:T(8,128)S(1)}, s32[]{:T(128)}, bf16[8,768,2240]{2,1,0:T(8,128)(2,1)}, s32[]{:T(128)}, /*index=5*/bf16[8,192,192]{2...) while((s32[]{:T(128)}, f32[768,192]{0,1:T(8,128)S(1)}, ...), condition=%wide.region_8.8_spmd.clone, body=%wide.region_7.7_spmd.clone.sunk | while | flops 56844292 | bytes 1672871 | solution.py:115
  242.5 9.1 %while.64 = (s32[]{:T(128)}, f32[768,192]{0,1:T(8,128)S(1)}, s32[]{:T(128)}, bf16[8,768,2240]{2,1,0:T(8,128)(2,1)}, s32[]{:T(128)}, /*index=5*/bf16[8,192,192]{2...) while((s32[]{:T(128)}, f32[768,192]{0,1:T(8,128)S(1)}, ...), condition=%wide.region_8.8_spmd.clone, body=%wide.region_7.7_spmd.clone.sunk | while | flops 56844292 | bytes 1672871 | solution.py:115
  260.8 9.1 %while.64 = (s32[]{:T(128)}, f32[768,192]{0,1:T(8,128)S(1)}, s32[]{:T(128)}, bf16[8,768,2240]{2,1,0:T(8,128)(2,1)}, s32[]{:T(128)}, /*index=5*/bf16[8,192,192]{2...) while((s32[]{:T(128)}, f32[768,192]{0,1:T(8,128)S(1)}, ...), condition=%wide.region_8.8_spmd.clone, body=%wide.region_7.7_spmd.clone.sunk | while | flops 56844292 | bytes 1672871 | solution.py:115
  279.1 9.1 %while.64 = (s32[]{:T(128)}, f32[768,192]{0,1:T(8,128)S(1)}, s32[]{:T(128)}, bf16[8,768,2240]{2,1,0:T(8,128)(2,1)}, s32[]{:T(128)}, /*index=5*/bf16[8,192,192]{2...) while((s32[]{:T(128)}, f32[768,192]{0,1:T(8,128)S(1)}, ...), condition=%wide.region_8.8_spmd.clone, body=%wide.region_7.7_spmd.clone.sunk | while | flops 56844292 | bytes 1672871 | solution.py:115
  297.4 9.1 %while.64 = (s32[]{:T(128)}, f32[768,192]{0,1:T(8,128)S(1)}, s32[]{:T(128)}, bf16[8,768,2240]{2,1,0:T(8,128)(2,1)}, s32[]{:T(128)}, /*index=5*/bf16[8,192,192]{2...) while((s32[]{:T(128)}, f32[768,192]{0,1:T(8,128)S(1)}, ...), condition=%wide.region_8.8_spmd.clone, body=%wide.region_7.7_spmd.clone.sunk | while | flops 56844292 | bytes 1672871 | solution.py:115
  315.6 9.1 %while.64 = (s32[]{:T(128)}, f32[768,192]{0,1:T(8,128)S(1)}, s32[]{:T(128)}, bf16[8,768,2240]{2,1,0:T(8,128)(2,1)}, s32[]{:T(128)}, /*index=5*/bf16[8,192,192]{2...) while((s32[]{:T(128)}, f32[768,192]{0,1:T(8,128)S(1)}, ...), condition=%wide.region_8.8_spmd.clone, body=%wide.region_7.7_spmd.clone.sunk | while | flops 56844292 | bytes 1672871 | solution.py:115
  333.9 9.1 %while.64 = (s32[]{:T(128)}, f32[768,192]{0,1:T(8,128)S(1)}, s32[]{:T(128)}, bf16[8,768,2240]{2,1,0:T(8,128)(2,1)}, s32[]{:T(128)}, /*index=5*/bf16[8,192,192]{2...) while((s32[]{:T(128)}, f32[768,192]{0,1:T(8,128)S(1)}, ...), condition=%wide.region_8.8_spmd.clone, body=%wide.region_7.7_spmd.clone.sunk | while | flops 56844292 | bytes 1672871 | solution.py:115
  352.2 9.1 %while.64 = (s32[]{:T(128)}, f32[768,192]{0,1:T(8,128)S(1)}, s32[]{:T(128)}, bf16[8,768,2240]{2,1,0:T(8,128)(2,1)}, s32[]{:T(128)}, /*index=5*/bf16[8,192,192]{2...) while((s32[]{:T(128)}, f32[768,192]{0,1:T(8,128)S(1)}, ...), condition=%wide.region_8.8_spmd.clone, body=%wide.region_7.7_spmd.clone.sunk | while | flops 56844292 | bytes 1672871 | solution.py:115
  370.5 9.1 %while.64 = (s32[]{:T(128)}, f32[768,192]{0,1:T(8,128)S(1)}, s32[]{:T(128)}, bf16[8,768,2240]{2,1,0:T(8,128)(2,1)}, s32[]{:T(128)}, /*index=5*/bf16[8,192,192]{2...) while((s32[]{:T(128)}, f32[768,192]{0,1:T(8,128)S(1)}, ...), condition=%wide.region_8.8_spmd.clone, body=%wide.region_7.7_spmd.clone.sunk | while | flops 56844292 | bytes 1672871 | solution.py:115
  388.8 9.1 %while.64 = (s32[]{:T(128)}, f32[768,192]{0,1:T(8,128)S(1)}, s32[]{:T(128)}, bf16[8,768,2240]{2,1,0:T(8,128)(2,1)}, s32[]{:T(128)}, /*index=5*/bf16[8,192,192]{2...) while((s32[]{:T(128)}, f32[768,192]{0,1:T(8,128)S(1)}, ...), condition=%wide.region_8.8_spmd.clone, body=%wide.region_7.7_spmd.clone.sunk | while | flops 56844292 | bytes 1672871 | solution.py:115
  407.1 9.1 %while.64 = (s32[]{:T(128)}, f32[768,192]{0,1:T(8,128)S(1)}, s32[]{:T(128)}, bf16[8,768,2240]{2,1,0:T(8,128)(2,1)}, s32[]{:T(128)}, /*index=5*/bf16[8,192,192]{2...) while((s32[]{:T(128)}, f32[768,192]{0,1:T(8,128)S(1)}, ...), condition=%wide.region_8.8_spmd.clone, body=%wide.region_7.7_spmd.clone.sunk | while | flops 56844292 | bytes 1672871 | solution.py:115
  425.3 9.1 %while.64 = (s32[]{:T(128)}, f32[768,192]{0,1:T(8,128)S(1)}, s32[]{:T(128)}, bf16[8,768,2240]{2,1,0:T(8,128)(2,1)}, s32[]{:T(128)}, /*index=5*/bf16[8,192,192]{2...) while((s32[]{:T(128)}, f32[768,192]{0,1:T(8,128)S(1)}, ...), condition=%wide.region_8.8_spmd.clone, body=%wide.region_7.7_spmd.clone.sunk | while | flops 56844292 | bytes 1672871 | solution.py:115
  443.6 9.1 %while.64 = (s32[]{:T(128)}, f32[768,192]{0,1:T(8,128)S(1)}, s32[]{:T(128)}, bf16[8,768,2240]{2,1,0:T(8,128)(2,1)}, s32[]{:T(128)}, /*index=5*/bf16[8,192,192]{2...) while((s32[]{:T(128)}, f32[768,192]{0,1:T(8,128)S(1)}, ...), condition=%wide.region_8.8_spmd.clone, body=%wide.region_7.7_spmd.clone.sunk | while | flops 56844292 | bytes 1672871 | solution.py:115
  456.9 5.8 slice.19
  462.7 6.6 copy.16
  472.1 245.3 %all-reduce.5.cloned.1.call-done = f32[4,192,2048]{2,1,0:T(8,128)} async-done(((f32[4,192,2048]{2,1,0:T(8,128)}), f32[4,192,2048]{2,1,0:T(8,128)}) %all-reduce.5.cloned.1.call-update) | async-done | bytes 6291472 | tf_op jit(solution)/shard_map/psum | solution.py:130
  717.4 4.7 fusion.49
  722.1 4.6 multiply_reduce_fusion
  726.7 9.3 %all_to_all.11 = f32[4,1,2]{2,1,0:T(1,128)S(1)} all-to-all(f32[4,1,2]{2,1,0:T(1,128)S(1)} %broadcast_in_dim.42), channel_id=1, replica_groups=mesh['ops'=32,'site'=4] {'site'}, dimensions={0} | all-to-all | bytes 64 | tf_op jit(solution)/shard_map/all_to_all | solution.py:16
  (225 shorter events, 246.6 us)
Async XLA Ops:
  15.4 6.6 copy-start.4
  15.4 15.0 %copy-start.5 = (s32[2048]{0:T(1024)S(1)}, s32[2048]{0:T(1024)}, u32[]{:S(2)}) copy-start(s32[2048]{0:T(1024)} %param.19) | copy-start | bytes 24580
  15.4 145.6 %all-to-all-start = ((bf16[4,8,4,192,192]{4,3,1,2,0:T(8,128)(2,1)}), bf16[4,8,4,192,192]{4,3,1,2,0:T(8,128)(2,1)}, u32[]{:S(2)}, u32[]{:S(2)}) async-start(bf16[4,8,4,192,192]{4,3,1,2,0:T(8,128)(2,1)} %stack.44), calls=%async_computation | async-start | bytes 25165824 | tf_op jit(solution)/shard_map/all_to_all | solution.py:10
  22.0 695.4 %all-reduce.5.cloned.1.call-start = ((), (), s32[]{:S(2)}) async-start(), calls=%async_computation.2 | async-start | bytes 12582912 | tf_op jit(solution)/shard_map/psum | solution.py:130
  469.3 2.7 copy-start.3
  469.3 248.1 %copy-start = (bf16[192,2048]{1,0:T(8,128)(2,1)S(1)}, bf16[192,2048]{1,0:T(8,128)(2,1)}, u32[]{:S(2)}) copy-start(bf16[192,2048]{1,0:T(8,128)(2,1)} %get-tuple-element.835) | copy-start | bytes 2359300
  469.3 248.1 %copy-start.1 = (bf16[192,2048]{1,0:T(8,128)(2,1)S(1)}, bf16[192,2048]{1,0:T(8,128)(2,1)}, u32[]{:S(2)}) copy-start(bf16[192,2048]{1,0:T(8,128)(2,1)} %get-tuple-element.836) | copy-start | bytes 2359300
  469.3 248.1 %copy-start.2 = (f32[2048]{0:T(1024)S(1)}, f32[2048]{0:T(1024)}, u32[]{:S(2)}) copy-start(f32[2048]{0:T(1024)} %param.22) | copy-start | bytes 24580
Sparse Core Ops, SparseCore 0:
  469.5 247.9 all-reduce.4
